TPU v7x, 32 devices: a whole 2x2x4 slice. The times are simulated.
32 devices in a mesh: seq: 8 (over z, core), fsdp: 4 (over y, x).
Axes of the slice: x: 2, y: 2, z: 4, core: 2. Of those that a mesh axis runs over, the one named last changes fastest.
Arguments:
- block_input: bfloat16 [8, 1472, 1152], P('fsdp', 'seq')
- key_mask: int32 [16, 736], P('fsdp'), may hold values from 0 to 1, as said below
- slot_flags: int32 [16], P('fsdp'), may hold values from 0 to 1, as said below
- norm1_gain: bfloat16 [1152], P('fsdp'), may hold values from 0.5 to 1.5
- norm1_bias: bfloat16 [1152], P('fsdp'), may hold values from -3 to 3
- qkv_weight: bfloat16 [1152, 3456], P('fsdp'), may hold values from -0.25 to 0.25
- query_bias: bfloat16 [1152], P('fsdp'), may hold values from -3 to 3
- value_bias: bfloat16 [1152], P('fsdp'), may hold values from -3 to 3
- proj_weight: bfloat16 [1152, 1152], P('fsdp'), may hold values from -0.375 to 0.375
- proj_bias: bfloat16 [1152], P('fsdp'), may hold values from -3 to 3
- norm2_gain: bfloat16 [1152], P('fsdp'), may hold values from 0.5 to 1.5
- norm2_bias: bfloat16 [1152], P('fsdp'), may hold values from -3 to 3
- up_weight: bfloat16 [1152, 4304], P('fsdp'), may hold values from -0.1875 to 0.1875
- up_bias: bfloat16 [4304], P('fsdp'), may hold values from -3 to 3
- down_weight: bfloat16 [4304, 1152], P(None, 'fsdp'), may hold values from -0.09375 to 0.09375
- down_bias: bfloat16 [1152], P('fsdp'), may hold values from -3 to 3
- out_grad: bfloat16 [8, 1472, 1152], P('fsdp', 'seq'), may hold values from -6 to 6
Outputs:
- block_output: bfloat16 [8, 1472, 1152], P('fsdp', 'seq')
- input_grad: float32 [8, 1472, 1152], P('fsdp', 'seq')
- norm1_gain_grad: float32 [1152], P('fsdp')
- norm1_bias_grad: float32 [1152], P('fsdp')
- qkv_weight_grad: float32 [1152, 3456], P('fsdp')
- query_bias_grad: float32 [1152], P('fsdp')
- value_bias_grad: float32 [1152], P('fsdp')
- proj_weight_grad: float32 [1152, 1152], P('fsdp')
- proj_bias_grad: float32 [1152], P('fsdp')
- norm2_gain_grad: float32 [1152], P('fsdp')
- norm2_bias_grad: float32 [1152], P('fsdp')
- up_weight_grad: float32 [1152, 4304], P('fsdp')
- up_bias_grad: float32 [4304], P('fsdp')
- down_weight_grad: float32 [4304, 1152], P(None, 'fsdp')
- down_bias_grad: float32 [1152], P('fsdp')
Inputs may be any that keep to these rules, and one draw needn't show every extreme that they name: `key_mask`: positions 729 and beyond are 0 in every slot; every position of a slot whose flag is 0 is 0. `slot_flags`: exactly max(1, 1) slots have flag 0, at places drawn from the seed.
All inputs are finite; a program needn't handle non-finite values.
Results may differ from a plain program's by a relative error of at most 0.012.
The roundings to bfloat16 on the way count: a program that leaves them out, or rounds other values in their place, can miss the bound.
Values may be sent and summed in bfloat16 or wider, within the bound.
A program may use at most 256 MiB of HBM per device.

v0:
```python
import jax
import jax.numpy as jnp
from jax import lax
from jax.sharding import Mesh
from jax.sharding import PartitionSpec as P

HEADS = 16
HEAD = 72
epsilon = 1e-06
SEQ = ("zh", "zl", "core")
ZAX = ("zh", "zl")
GROUP = ("zl", "core")


def layer_norm(values, gain_vec, bias_vec):
    row_mean = jnp.mean(values, axis=-1, keepdims=True)
    centered = values - row_mean
    variance = jnp.mean(centered * centered, axis=-1, keepdims=True)
    return centered * lax.rsqrt(variance + epsilon) * gain_vec + bias_vec


def gelu_tanh(values):
    return (
        0.5
        * values
        * (1.0 + jnp.tanh(0.7978845608028654 * (values + 0.044715 * values * values * values)))
    )


def core_swap(x):
    return lax.ppermute(x, "core", [(0, 1), (1, 0)])


def in_core_order(mine, other):
    first = lax.axis_index("core") == 0
    return (jnp.where(first, mine, other), jnp.where(first, other, mine))


def gather_weight(w):
    rows, cols = w.shape
    half = rows // 2
    piece = lax.dynamic_slice_in_dim(w, lax.axis_index("core") * half, half, axis=0)
    mine = lax.all_gather(piece, "fsdp", axis=0, tiled=False)
    other = core_swap(mine)
    first, second = in_core_order(mine, other)
    return jnp.stack([first, second], axis=1).reshape(-1, cols)


def reduce_weight(g):
    rows, cols = g.shape
    fsdp = lax.axis_size("fsdp")
    blocks = g.reshape(fsdp, 2, rows // (2 * fsdp), cols)
    core = lax.axis_index("core")
    mine = lax.dynamic_index_in_dim(blocks, core, axis=1, keepdims=False)
    other = lax.dynamic_index_in_dim(blocks, 1 - core, axis=1, keepdims=False)
    chip = mine + core_swap(other.astype(jnp.bfloat16)).astype(jnp.float32)
    part = lax.psum_scatter(chip.astype(jnp.bfloat16), "fsdp", scatter_dimension=0, tiled=True)
    part = lax.psum(part, ZAX).astype(jnp.float32)
    first, second = in_core_order(part, core_swap(part))
    return jnp.concatenate([first[0], second[0]], axis=0)


def shards(
    block_input,
    key_mask,
    slot_flags,
    norm1_gain,
    norm1_bias,
    qkv_weight,
    query_bias,
    value_bias,
    proj_weight,
    proj_bias,
    norm2_gain,
    norm2_bias,
    up_weight,
    up_bias,
    down_weight,
    down_bias,
    out_grad,
):
    f32, bf16 = (jnp.float32, jnp.bfloat16)
    pairs, part_rows, width = block_input.shape
    group = lax.axis_size("zl") * lax.axis_size("core")
    local_heads = HEADS // group
    slot_len = part_rows * group
    zh = lax.axis_index("zh")
    scale = HEAD ** (-0.5)
    vectors = (
        norm1_gain,
        norm1_bias,
        query_bias,
        value_bias,
        proj_bias,
        norm2_gain,
        norm2_bias,
        up_bias,
        down_bias,
    )
    sizes = [v.shape[0] for v in vectors]
    packed = jnp.concatenate([v.astype(f32) for v in vectors])
    packed = lax.all_gather(packed, "fsdp", axis=0, tiled=False)
    full_vectors = []
    at = 0
    for n in sizes:
        full_vectors.append(packed[:, at : at + n].reshape(-1))
        at += n
    g1, b1, bq, bv, bproj, g2, b2, bup, bdown = full_vectors
    w_qkv = gather_weight(qkv_weight)
    w_proj = gather_weight(proj_weight)
    w_up = gather_weight(up_weight)
    w_down_t = gather_weight(down_weight.T)
    flags = slot_flags.astype(f32).reshape(pairs, 2)
    row_flags = lax.dynamic_index_in_dim(flags, zh, axis=1, keepdims=False)
    live = lax.dynamic_index_in_dim(key_mask.reshape(pairs, 2, -1), zh, axis=1, keepdims=False)
    mask_bias = (live.astype(f32) - 1.0) * 10000.0
    rows = block_input.reshape(pairs * part_rows, width).astype(f32)
    normed, norm_one_back = jax.vjp(layer_norm, rows, g1, b1)
    normed_low = normed.astype(bf16)
    mixed = jnp.dot(normed_low, w_qkv, preferred_element_type=f32)
    q = (mixed[:, :width] + bq).astype(bf16)
    k = mixed[:, width : 2 * width].astype(bf16)
    v = (mixed[:, 2 * width :] + bv).astype(bf16)
    qkv_tok = jnp.stack([q, k, v]).reshape(3, pairs, part_rows, width)
    qkv_heads = lax.all_to_all(qkv_tok, GROUP, split_axis=3, concat_axis=2, tiled=True)
    qkv_heads = qkv_heads.reshape(3, pairs, slot_len, local_heads, HEAD)
    qh, kh, vh = (qkv_heads[0], qkv_heads[1], qkv_heads[2])
    scores = jnp.einsum("pqhd,pkhd->phqk", qh, kh, preferred_element_type=f32) * scale
    shifted = scores + mask_bias[:, None, None, :]
    row_max = jnp.max(shifted, axis=-1, keepdims=True)
    exp_terms = jnp.exp(shifted - row_max)
    probs = exp_terms / jnp.sum(exp_terms, axis=-1, keepdims=True)
    weights_low = probs.astype(bf16)
    attended = jnp.einsum("phqk,pkhd->pqhd", weights_low, vh, preferred_element_type=f32)
    attended = attended.astype(bf16).reshape(pairs, slot_len, local_heads * HEAD)
    merged = lax.all_to_all(attended, GROUP, split_axis=1, concat_axis=2, tiled=True)
    merged_rows = merged.reshape(pairs * part_rows, width)
    hidden = rows + jnp.dot(merged_rows, w_proj, preferred_element_type=f32) + bproj
    second, norm_two_back = jax.vjp(layer_norm, hidden, g2, b2)
    second_low = second.astype(bf16)
    gate_in = jnp.dot(second_low, w_up, preferred_element_type=f32) + bup
    active, gelu_back = jax.vjp(gelu_tanh, gate_in)
    active_low = active.astype(bf16)
    result = (
        hidden
        + lax.dot_general(
            active_low, w_down_t, (((1,), (1,)), ((), ())), preferred_element_type=f32
        )
        + bdown
    )
    row_flag_rows = jnp.repeat(row_flags, part_rows)[:, None]
    output = (result * row_flag_rows).astype(bf16).reshape(pairs, part_rows, width)
    grad_rows = out_grad.reshape(pairs * part_rows, width).astype(f32) * row_flag_rows
    grad_low = grad_rows.astype(bf16)
    down_weight_grad_t = jnp.dot(grad_low.T, active_low, preferred_element_type=f32)
    down_bias_grad = jnp.sum(grad_rows, axis=0)
    grad_active = jnp.dot(grad_low, w_down_t, preferred_element_type=f32)
    grad_gate = gelu_back(grad_active)[0].astype(bf16)
    up_weight_grad = jnp.dot(second_low.T, grad_gate, preferred_element_type=f32)
    up_bias_grad = jnp.sum(grad_gate.astype(f32), axis=0)
    grad_second = jnp.dot(grad_gate, w_up.T, preferred_element_type=f32)
    grad_hidden_norm, norm2_gain_grad, norm2_bias_grad = norm_two_back(grad_second)
    grad_hidden = grad_rows + grad_hidden_norm
    grad_branch = grad_hidden.astype(bf16)
    proj_weight_grad = jnp.dot(merged_rows.T, grad_branch, preferred_element_type=f32)
    proj_bias_grad = jnp.sum(grad_branch.astype(f32), axis=0)
    grad_merged = jnp.dot(grad_branch, w_proj.T, preferred_element_type=f32).astype(bf16)
    grad_heads = lax.all_to_all(
        grad_merged.reshape(pairs, part_rows, width), GROUP, split_axis=2, concat_axis=1, tiled=True
    ).reshape(pairs, slot_len, local_heads, HEAD)
    grad_probs = jnp.einsum("pqhd,pkhd->phqk", grad_heads, vh, preferred_element_type=f32)
    row_dot = jnp.sum(probs * grad_probs, axis=-1, keepdims=True)
    grad_scores = (probs * (grad_probs - row_dot)).astype(bf16)
    dq = (
        jnp.einsum("phqk,pkhd->pqhd", grad_scores, kh, preferred_element_type=f32) * scale
    ).astype(bf16)
    dk = (
        jnp.einsum("phqk,pqhd->pkhd", grad_scores, qh, preferred_element_type=f32) * scale
    ).astype(bf16)
    dv = jnp.einsum("phqk,pqhd->pkhd", weights_low, grad_heads, preferred_element_type=f32).astype(
        bf16
    )
    dqkv = jnp.stack([dq, dk, dv]).reshape(3, pairs, slot_len, local_heads * HEAD)
    dqkv_tok = lax.all_to_all(dqkv, GROUP, split_axis=2, concat_axis=3, tiled=True)
    dqkv_tok = dqkv_tok.reshape(3, pairs * part_rows, width)
    grad_mixed = jnp.concatenate([dqkv_tok[0], dqkv_tok[1], dqkv_tok[2]], axis=1)
    qkv_weight_grad = jnp.dot(normed_low.T, grad_mixed, preferred_element_type=f32)
    query_bias_grad = jnp.sum(dqkv_tok[0].astype(f32), axis=0)
    value_bias_grad = jnp.sum(dqkv_tok[2].astype(f32), axis=0)
    grad_normed = jnp.dot(grad_mixed, w_qkv.T, preferred_element_type=f32)
    grad_rows_norm, norm1_gain_grad, norm1_bias_grad = norm_one_back(grad_normed)
    input_grad = (grad_hidden + grad_rows_norm).reshape(pairs, part_rows, width)
    vec_grads = (
        norm1_gain_grad,
        norm1_bias_grad,
        query_bias_grad,
        value_bias_grad,
        proj_bias_grad,
        norm2_gain_grad,
        norm2_bias_grad,
        up_bias_grad,
        down_bias_grad,
    )
    fsdp = lax.axis_size("fsdp")
    stacked = jnp.concatenate([g.reshape(fsdp, -1) for g in vec_grads], axis=1)
    stacked = lax.psum_scatter(stacked, "fsdp", scatter_dimension=0, tiled=True)
    stacked = lax.psum(stacked, SEQ).reshape(-1)
    vec_out = []
    at = 0
    for g in vec_grads:
        n = g.shape[0] // fsdp
        vec_out.append(stacked[at : at + n])
        at += n
    n1g, n1b, qb, vb, pb, n2g, n2b, ub, db = vec_out
    down_g = reduce_weight(down_weight_grad_t).T
    up_g = reduce_weight(up_weight_grad)
    proj_g = reduce_weight(proj_weight_grad)
    qkv_g = reduce_weight(qkv_weight_grad)
    return (output, input_grad, n1g, n1b, qkv_g, qb, vb, proj_g, pb, n2g, n2b, up_g, ub, down_g, db)


def solution(mesh):
    seq_n = mesh.shape["seq"]
    fsdp_n = mesh.shape["fsdp"]
    devices = mesh.devices.reshape(2, seq_n // 4, 2, fsdp_n)
    inner = Mesh(devices, ("zh", "zl", "core", "fsdp"))
    tok = P("fsdp", SEQ, None)
    vec = P("fsdp")
    rows = P("fsdp", None)
    in_specs = (
        tok,
        rows,
        vec,
        vec,
        vec,
        rows,
        vec,
        vec,
        rows,
        vec,
        vec,
        vec,
        rows,
        vec,
        P(None, "fsdp"),
        vec,
        tok,
    )
    out_specs = (
        tok,
        tok,
        vec,
        vec,
        rows,
        vec,
        vec,
        rows,
        vec,
        vec,
        vec,
        rows,
        vec,
        P(None, "fsdp"),
        vec,
    )
    return jax.shard_map(
        shards, mesh=inner, in_specs=in_specs, out_specs=out_specs, check_vma=False
    )
```

profile of v0, /device:TPU:0, one launch (start us, length us, event | category | flops | bytes accessed | tf_op | source)
XLA Modules:
  0.0 1008.7 jit_solution(17743258620124356132)
XLA Ops:
  14.5 49.5 %all-gather.10.cloned.1.call-done = bf16[576,3456]{1,0:T(8,128)(2,1)} async-done(((bf16[144,3456]{1,0:T(8,128)(2,1)}), bf16[576,3456]{1,0:T(8,128)(2,1)}) %all-gather.10.cloned.1.call-update) | async-done | bytes 3981328 | tf_op jit(solution)/shard_map/all_gather | solution.py:43
  65.6 16.9 %all-reduce = f32[13520]{0:T(1024)S(1)} all-reduce(f32[13520]{0:T(1024)S(1)} %convert_dynamic-update-slice_fusion), channel_id=2, replica_groups=mesh['zh'=2,'zl'=2,'core'=2,'fsdp'=4] {'fsdp'}, use_global_device_ids=true, to_apply=%add | all-reduce | flops 13520 | bytes 108160
  87.9 7.8 all-gather.12.cloned.1.call-done
  95.6 61.8 %all-gather.16.cloned.1.call-done = bf16[576,4304]{1,0:T(8,128)(2,1)} async-done(((bf16[144,4304]{1,0:T(8,128)(2,1)}), bf16[576,4304]{1,0:T(8,128)(2,1)}) %all-gather.16.cloned.1.call-update) | async-done | bytes 4958224 | tf_op jit(solution)/shard_map/all_gather | solution.py:43
  157.5 61.7 %all-gather.14.cloned.1.call-done = bf16[576,4304]{1,0:T(8,128)(2,1)} async-done(((bf16[144,4304]{1,0:T(8,128)(2,1)}), bf16[576,4304]{1,0:T(8,128)(2,1)}) %all-gather.14.cloned.1.call-update) | async-done | bytes 4958224 | tf_op jit(solution)/shard_map/all_gather | solution.py:43
  219.2 5.0 select_bitcast_fusion.5
  224.2 6.1 pad_maximum_fusion.2
  230.2 6.0 fusion.65
  250.5 8.5 pad_maximum_fusion.5
  258.9 4.9 all-to-all-start
  267.6 8.5 select_bitcast_fusion.1
  276.1 8.3 select_bitcast_fusion.3
  284.4 20.6 %all-to-all-done = bf16[3,2,184,1152]{2,1,0,3:T(2,128)(2,1)} async-done(((bf16[3,2,184,1152]{2,1,0,3:T(2,128)(2,1)}), bf16[3,2,184,1152]{2,1,0,3:T(2,128)(2,1)}, u32[]{:S(2)}, u32[]{:S(2)}) %all-to-all-start) | async-done | bytes 2543648 | tf_op jit(solution)/shard_map/all_to_all | solution.py:125
  305.0 12.6 %copy.128 = bf16[3,2,184,4,288]{4,3,2,1,0:T(4,128)(2,1)} copy(bf16[3,2,184,4,288]{2,1,0,4,3:T(2,128)(2,1)} %bitcast.11) | data formatting | bytes 5087232 | tf_op jit(solution)/shard_map/all_to_all | solution.py:125
  339.0 10.8 %fusion.63 = (f32[2,4,736]{2,1,0:T(4,128)S(1)}, f32[2,4,736,736]{2,3,1,0:T(8,128)}) fusion(f32[2,736]{1,0:T(2,128)S(1)} %fusion.49, bf16[2,736,4,72]{1,3,2,0:T(8,128)(2,1)} %squeeze.70, bf16[2,736,4,72]{1,3,2,0:T(8,128)(2,1)S(1)} %squeeze.71), kind=kOutput, calls=%fused_computation.161 | convolution fusion | flops 641368768 | bytes 19059456 | tf_op jit(solution)/shard_map/sub | solution.py:131
  349.7 9.1 fusion.34
  358.8 4.7 copy.95
  367.8 8.7 pad_maximum_fusion
  376.5 8.3 copy.99
  384.8 8.6 pad_maximum_fusion.1
  402.7 8.4 convolution_add_fusion
  411.2 10.9 %convert_reduce_fusion = (f32[4304]{0:T(1024)}, bf16[368,4304]{1,0:T(8,128)(2,1)}) fusion(f32[368,4304]{1,0:T(8,128)S(1)} %convolution_add_fusion, bf16[368,1152]{1,0:T(8,128)(2,1)S(1)} %bitcast.232, bf16[1152,4304]{1,0:T(8,128)(2,1)S(1)} %bitcast.202), kind=kOutput, calls=%fused_computation.32 | convolution fusion | flops 3690417408 | bytes 20284736 | tf_op jit(solution)/shard_map/dot_general | solution.py:157
  422.1 10.1 multiply_reduce_fusion.1
  432.2 10.0 fusion.54
  465.3 6.6 fusion.13
  478.4 12.3 %multiply_reduce_fusion = (f32[2,4,736]{2,1,0:T(4,128)S(1)}, f32[2,4,736,736]{2,3,1,0:T(8,128)}) fusion(f32[2,4,736,736]{2,3,1,0:T(8,128)} %get-tuple-element.83, f32[2,4,736]{2,1,0:T(4,128)S(1)} %get-tuple-element.82, bf16[2,736,4,72]{1,3,2,0:T(8,128)(2,1)} %reshape.304, bf16[2,736,4,72]{1,3,2,0:T(8,128)(2,1)} %squeeze.69), kind=kOutput, calls=%fused_computation.2 | convolution fusion | flops 637028608 | bytes 36411392 | tf_op jit(solution)/shard_map/pqhd,pkhd->phqk/dot_general | solution.py:171
  490.6 12.3 %multiply_convert_fusion = bf16[2,4,736,736]{2,3,1,0:T(8,128)(2,1)S(1)} fusion(f32[2,4,736,736]{2,3,1,0:T(8,128)} %get-tuple-element.88, f32[2,4,736]{2,1,0:T(4,128)S(1)} %get-tuple-element.87, f32[2,4,736,736]{2,3,1,0:T(8,128)} %get-tuple-element.83, f32[2,4,736]{2,1,0:T(4,128)S(1)} %get-tuple-element.82), kind=kLoop, calls=%fused_computation.1 | loop fusion | flops 17334272 | bytes 43382784 | tf_op jit(solution)/shard_map/convert_element_type | solution.py:173
  503.0 9.9 fusion.37
  519.2 4.7 copy.109
  523.9 4.9 copy.108
  531.6 8.7 pad_maximum_fusion.6
  540.3 4.7 all-to-all-start.3
  548.6 8.7 fusion.3
  559.5 25.1 %all-to-all-done.3 = bf16[3,2,736,288]{3,1,0,2:T(2,128)(2,1)} async-done(((bf16[3,2,736,288]{3,1,0,2:T(2,128)(2,1)}), bf16[3,2,736,288]{3,1,0,2:T(2,128)(2,1)}, u32[]{:S(2)}, u32[]{:S(2)}) %all-to-all-start.3) | async-done | bytes 2543648 | tf_op jit(solution)/shard_map/all_to_all | solution.py:184
  584.6 12.9 %copy.133 = bf16[3,2,4,184,288]{3,2,4,1,0:T(4,128)(2,1)} copy(bf16[3,2,4,184,288]{4,1,0,3,2:T(2,128)(2,1)} %bitcast.47) | data formatting | bytes 5087232 | tf_op jit(solution)/shard_map/all_to_all | solution.py:184
  622.7 7.4 fusion.66
  634.1 6.1 fusion.27
  640.2 5.5 copy-done.2
  656.8 7.1 fusion.6
  664.0 12.5 %fusion.20 = f32[4,2,144,4304]{3,2,1,0:T(8,128)} fusion(bf16[4,2,144,368]{3,2,1,0:T(8,128)(2,1)S(1)} %bitcast.207, f32[368,4304]{1,0:T(8,128)} %copy-done.13), kind=kOutput, calls=%fused_computation.52 | convolution fusion | flops 3663495936 | bytes 27016192 | tf_op jit(solution)/shard_map/dot_general | solution.py:155
  682.0 8.1 collective-permute-done.10
  690.1 8.9 fusion.2
  699.2 15.0 %reduce-scatter.13.cloned.1.call-done = bf16[1,144,3456]{2,1,0:T(8,128)(2,1)} async-done(((bf16[4,144,3456]{2,1,0:T(8,128)(2,1)}), bf16[1,144,3456]{2,1,0:T(8,128)(2,1)}) %reduce-scatter.13.cloned.1.call-update) | async-done | bytes 995344
  714.2 63.1 %reduce-scatter.19.cloned.1.call-done = bf16[1,144,4304]{2,1,0:T(8,128)(2,1)} async-done(((bf16[4,144,4304]{2,1,0:T(8,128)(2,1)}), bf16[1,144,4304]{2,1,0:T(8,128)(2,1)}) %reduce-scatter.19.cloned.1.call-update) | async-done | bytes 1239568
  777.5 145.8 %all-reduce.9.cloned.1.call-done = (bf16[1,144,3456]{2,1,0:T(8,128)(2,1)}, bf16[1,144,1152]{2,1,0:T(8,128)(2,1)}, bf16[1,144,4304]{2,1,0:T(8,128)(2,1)}, bf16[1,144,4304]{2,1,0:T(8,128)(2,1)}) async-done(((bf16[1,144,3456]{2,1,0:T(8,128)(2,1)}, bf16[1,144,1152]{2,1,0:T(8,128)(2,1)}, bf16[1,144,4304]{2,1,0:T(8,128)(2,1)}, bf16[1,144,4304]{2,1,0:T(8,128)(2,1)}), (bf16[1,144,3456]{2,1,0:T(8,128)(2,1)}, ...) | async-done | bytes 3806224 | tf_op jit(solution)/shard_map/psum | solution.py:58
  926.1 11.2 %fusion.25 = bf16[368,1152]{1,0:T(8,128)(2,1)} fusion(f32[368,1152]{1,0:T(8,128)S(1)} %copy-done.6, bf16[1152,4304]{1,0:T(8,128)(2,1)} %bitcast.199, f32[368]{0:T(512)S(1)} %mul.257, f32[1152]{0:T(1024)S(1)} %add.220, f32[368,4304]{1,0:T(8,128)} %copy-done.13), kind=kOutput, calls=%fused_computation.59 | convolution fusion | flops 3665191680 | bytes 18801600 | tf_op jit(solution)/shard_map/dot_general | solution.py:146
  941.0 17.7 %all-reduce.1 = f32[4,3380]{1,0:T(4,128)} all-reduce(f32[4,3380]{1,0:T(4,128)S(1)} %concatenate.26), channel_id=7, replica_groups=mesh['zh'=2,'zl'=2,'core'=2,'fsdp'=4] {'fsdp'}, use_global_device_ids=true, to_apply=%region_20.21.clone | all-reduce | flops 13520 | bytes 108160
  961.1 27.2 %psum.35 = f32[1,3380]{1,0:T(1,128)S(1)} all-reduce(f32[1,3380]{1,0:T(1,128)S(1)} %constant_dynamic-slice_fusion.5), channel_id=1, replica_groups=mesh['zh'=2,'zl'=2,'core'=2,'fsdp'=4] {'zh','zl','core'}, use_global_device_ids=true, to_apply=%region_21.22 | all-reduce | flops 3380 | bytes 27040 | tf_op jit(solution)/shard_map/psum | solution.py:207
  (284 shorter events, 179.2 us)
Async XLA Ops:
  7.2 56.8 %all-gather.10.cloned.1.call-start = ((), (), s32[]{:S(2)}) async-start(), calls=%async_computation.8 | async-start | bytes 4976640 | tf_op jit(solution)/shard_map/all_gather | solution.py:43
  9.7 85.9 %all-gather.12.cloned.1.call-start = ((), (), s32[]{:S(2)}) async-start(), calls=%async_computation.9 | async-start | bytes 1658880 | tf_op jit(solution)/shard_map/all_gather | solution.py:43
  10.5 146.9 %all-gather.16.cloned.1.call-start = ((), (), s32[]{:S(2)}) async-start(), calls=%async_computation.11 | async-start | bytes 6266880 | tf_op jit(solution)/shard_map/all_gather | solution.py:43
  11.7 52.3 %copy-start.46 = (u32[32]{0:T(128)S(1)}, u32[32]{0:T(128)}, u32[]{:S(2)}) copy-start(u32[32]{0:T(128)} %constant.89) | copy-start | bytes 388
  11.7 53.5 %copy-start.45 = (bf16[1076]{0:T(1024)(128)(2,1)S(1)}, bf16[1076]{0:T(1024)(128)(2,1)}, u32[]{:S(2)}) copy-start(bf16[1076]{0:T(1024)(128)(2,1)} %param.30) | copy-start | bytes 6460
  11.7 53.5 %copy-start.47 = (bf16[288]{0:T(512)(128)(2,1)S(1)}, bf16[288]{0:T(512)(128)(2,1)}, u32[]{:S(2)}) copy-start(bf16[288]{0:T(512)(128)(2,1)} %param.20) | copy-start | bytes 1732
  11.7 53.5 %copy-start.48 = (bf16[288]{0:T(512)(128)(2,1)S(1)}, bf16[288]{0:T(512)(128)(2,1)}, u32[]{:S(2)}) copy-start(bf16[288]{0:T(512)(128)(2,1)} %param.21) | copy-start | bytes 1732
  11.7 53.5 %copy-start.49 = (bf16[288]{0:T(512)(128)(2,1)S(1)}, bf16[288]{0:T(512)(128)(2,1)}, u32[]{:S(2)}) copy-start(bf16[288]{0:T(512)(128)(2,1)} %param.23) | copy-start | bytes 1732
  11.8 53.5 %copy-start.50 = (bf16[288]{0:T(512)(128)(2,1)S(1)}, bf16[288]{0:T(512)(128)(2,1)}, u32[]{:S(2)}) copy-start(bf16[288]{0:T(512)(128)(2,1)} %param.24) | copy-start | bytes 1732
  11.8 53.5 %copy-start.51 = (bf16[288]{0:T(512)(128)(2,1)S(1)}, bf16[288]{0:T(512)(128)(2,1)}, u32[]{:S(2)}) copy-start(bf16[288]{0:T(512)(128)(2,1)} %param.26) | copy-start | bytes 1732
  11.8 53.5 %copy-start.52 = (bf16[288]{0:T(512)(128)(2,1)S(1)}, bf16[288]{0:T(512)(128)(2,1)}, u32[]{:S(2)}) copy-start(bf16[288]{0:T(512)(128)(2,1)} %param.27) | copy-start | bytes 1732
  11.8 53.5 %copy-start.53 = (bf16[288]{0:T(512)(128)(2,1)S(1)}, bf16[288]{0:T(512)(128)(2,1)}, u32[]{:S(2)}) copy-start(bf16[288]{0:T(512)(128)(2,1)} %param.28) | copy-start | bytes 1732
  11.8 53.5 %copy-start.54 = (bf16[288]{0:T(512)(128)(2,1)S(1)}, bf16[288]{0:T(512)(128)(2,1)}, u32[]{:S(2)}) copy-start(bf16[288]{0:T(512)(128)(2,1)} %param.32) | copy-start | bytes 1732
  11.8 71.9 %copy-start.41 = (s32[4,736]{1,0:T(4,128)S(1)}, s32[4,736]{1,0:T(4,128)}, u32[]{:S(2)}) copy-start(s32[4,736]{1,0:T(4,128)} %param.18) | copy-start | bytes 35332
  11.8 71.9 %copy-start.55 = (s32[4]{0:T(128)S(1)}, s32[4]{0:T(128)}, u32[]{:S(2)}) copy-start(s32[4]{0:T(128)} %param.19) | copy-start | bytes 52
  11.8 72.6 %copy-start.3 = (bf16[2,184,1152]{2,1,0:T(8,128)(2,1)S(1)}, bf16[2,184,1152]{2,1,0:T(8,128)(2,1)}, u32[]{:S(2)}) copy-start(bf16[2,184,1152]{2,1,0:T(8,128)(2,1)} %param.17) | copy-start | bytes 2543620
  11.9 73.8 %copy-start.9 = (bf16[2,184,1152]{2,1,0:T(8,128)(2,1)S(1)}, bf16[2,184,1152]{2,1,0:T(8,128)(2,1)}, u32[]{:S(2)}) copy-start(bf16[2,184,1152]{2,1,0:T(8,128)(2,1)} %param.33) | copy-start | bytes 2543620
  11.9 207.3 %all-gather.14.cloned.1.call-start = ((), (), s32[]{:S(2)}) async-start(), calls=%async_computation.10 | async-start | bytes 6266880 | tf_op jit(solution)/shard_map/all_gather | solution.py:43
  64.0 155.2 %collective-permute-start = (bf16[4,144,3456]{2,1,0:T(8,128)(2,1)}, bf16[4,144,3456]{2,1,0:T(8,128)(2,1)}, u32[]{:S(2)}, u32[]{:S(2)}) collective-permute-start(bf16[4,144,3456]{2,1,0:T(8,128)(2,1)} %bitcast.215), channel_id=1, source_target_pairs={{0,4},{4,0},{1,5},{5,1},{2,6},{6,2},{3,7},{7,3},{8,12},{12,8},{9,1... | collective-permute-start | bytes 11943944 | tf_op jit(solution)/shard_map/ppermute | solution.py:31
  84.7 139.5 %copy-start.36 = (f32[2,184]{1,0:T(2,128)}, f32[2,184]{1,0:T(2,128)S(1)}, u32[]{:S(2)}) copy-start(f32[2,184]{1,0:T(2,128)S(1)} %broadcast_multiply_fusion.1) | copy-start | bytes 4420
  95.6 168.2 %collective-permute-start.1 = (bf16[4,144,1152]{2,1,0:T(8,128)(2,1)}, bf16[4,144,1152]{2,1,0:T(8,128)(2,1)}, u32[]{:S(2)}, u32[]{:S(2)}) collective-permute-start(bf16[4,144,1152]{2,1,0:T(8,128)(2,1)} %bitcast.228), channel_id=1, source_target_pairs={{0,4},{4,0},{1,5},{5,1},{2,6},{6,2},{3,7},{7,3},{8,12},{12,8},{9,1... | collective-permute-start | bytes 3981320 | tf_op jit(solution)/shard_map/ppermute | solution.py:31
  157.5 110.1 %collective-permute-start.3 = (bf16[4,144,4304]{2,1,0:T(8,128)(2,1)}, bf16[4,144,4304]{2,1,0:T(8,128)(2,1)}, u32[]{:S(2)}, u32[]{:S(2)}) collective-permute-start(bf16[4,144,4304]{2,1,0:T(8,128)(2,1)} %bitcast.209), channel_id=1, source_target_pairs={{0,4},{4,0},{1,5},{5,1},{2,6},{6,2},{3,7},{7,3},{8,12},{12,8},{9,1... | collective-permute-start | bytes 14874632 | tf_op jit(solution)/shard_map/ppermute | solution.py:31
  219.2 56.9 %collective-permute-start.2 = (bf16[4,144,4304]{2,1,0:T(8,128)(2,1)}, bf16[4,144,4304]{2,1,0:T(8,128)(2,1)}, u32[]{:S(2)}, u32[]{:S(2)}) collective-permute-start(bf16[4,144,4304]{2,1,0:T(8,128)(2,1)} %bitcast.211), channel_id=1, source_target_pairs={{0,4},{4,0},{1,5},{5,1},{2,6},{6,2},{3,7},{7,3},{8,12},{12,8},{9,1... | collective-permute-start | bytes 14874632 | tf_op jit(solution)/shard_map/ppermute | solution.py:31
  258.9 46.0 %all-to-all-start = ((bf16[3,2,184,1152]{2,1,0,3:T(2,128)(2,1)}), bf16[3,2,184,1152]{2,1,0,3:T(2,128)(2,1)}, u32[]{:S(2)}, u32[]{:S(2)}) async-start(bf16[3,2,184,1152]{2,1,0,3:T(2,128)(2,1)} %pad_maximum_fusion.5), calls=%async_computation | async-start | bytes 7077888 | tf_op jit(solution)/shard_map/all_to_all | solution.py:125
  363.5 29.9 %all-to-all-start.1 = ((bf16[2,736,288]{2,0,1:T(2,128)(2,1)}), bf16[2,736,288]{2,0,1:T(2,128)(2,1)}, u32[]{:S(2)}, u32[]{:S(2)}) async-start(bf16[2,736,288]{2,0,1:T(2,128)(2,1)} %copy.95), calls=%async_computation.1 | async-start | bytes 2260992 | tf_op jit(solution)/shard_map/all_to_all | solution.py:136
  402.3 39.8 %copy-start.5 = (f32[368,1152]{1,0:T(8,128)}, f32[368,1152]{1,0:T(8,128)S(1)}, u32[]{:S(2)}) copy-start(f32[368,1152]{1,0:T(8,128)S(1)} %get-tuple-element.85) | copy-start | bytes 5087236
  451.6 20.4 %all-to-all-start.2 = ((bf16[2,184,1152]{1,0,2:T(2,128)(2,1)}), bf16[2,184,1152]{1,0,2:T(2,128)(2,1)}, u32[]{:S(2)}, u32[]{:S(2)}) async-start(bf16[2,184,1152]{1,0,2:T(2,128)(2,1)} %copy.101), calls=%async_computation.2 | async-start | bytes 2359296 | tf_op jit(solution)/shard_map/all_to_all | solution.py:168
  464.8 80.3 %collective-permute-start.6 = (bf16[4,144,1152]{2,1,0:T(8,128)(2,1)}, bf16[4,144,1152]{2,1,0:T(8,128)(2,1)}, u32[]{:S(2)}, u32[]{:S(2)}) collective-permute-start(bf16[4,144,1152]{2,1,0:T(8,128)(2,1)} %fusion.40), channel_id=1, source_target_pairs={{0,4},{4,0},{1,5},{5,1},{2,6},{6,2},{3,7},{7,3},{8,12},{12,8},{9,1... | collective-permute-start | bytes 3981320 | tf_op jit(solution)/shard_map/ppermute | solution.py:31
  471.9 76.7 %collective-permute-start.8 = (bf16[4,144,4304]{2,1,0:T(8,128)(2,1)}, bf16[4,144,4304]{2,1,0:T(8,128)(2,1)}, u32[]{:S(2)}, u32[]{:S(2)}) collective-permute-start(bf16[4,144,4304]{2,1,0:T(8,128)(2,1)} %fusion.13), channel_id=1, source_target_pairs={{0,4},{4,0},{1,5},{5,1},{2,6},{6,2},{3,7},{7,3},{8,12},{12,8},{9,1... | collective-permute-start | bytes 14874632 | tf_op jit(solution)/shard_map/ppermute | solution.py:31
  490.6 12.3 %copy-start.28 = (bf16[2,736,4,72]{1,3,2,0:T(8,128)(2,1)S(1)}, bf16[2,736,4,72]{1,3,2,0:T(8,128)(2,1)}, u32[]{:S(2)}) copy-start(bf16[2,736,4,72]{1,3,2,0:T(8,128)(2,1)} %reshape.304) | copy-start | bytes 2543620
  540.3 44.3 %all-to-all-start.3 = ((bf16[3,2,736,288]{3,1,0,2:T(2,128)(2,1)}), bf16[3,2,736,288]{3,1,0,2:T(2,128)(2,1)}, u32[]{:S(2)}, u32[]{:S(2)}) async-start(bf16[3,2,736,288]{3,1,0,2:T(2,128)(2,1)} %pad_maximum_fusion.6), calls=%async_computation.3 | async-start | bytes 6782976 | tf_op jit(solution)/shard_map/all_to_all | solution.py:184
  545.0 154.2 %reduce-scatter.15.cloned.1.call-start = ((), (), s32[]{:S(2)}) async-start(), calls=%async_computation.13 | async-start | bytes 1658880
  548.5 150.7 %reduce-scatter.17.cloned.1.call-start = ((), (), s32[]{:S(2)}) async-start(), calls=%async_computation.14 | async-start | bytes 6266880
  557.3 156.9 %reduce-scatter.13.cloned.1.call-start = ((), (), s32[]{:S(2)}) async-start(), calls=%async_computation.12 | async-start | bytes 4976640
  648.1 8.7 collective-permute-start.4
  663.9 113.4 %reduce-scatter.19.cloned.1.call-start = ((), (), s32[]{:S(2)}) async-start(), calls=%async_computation.15 | async-start | bytes 6266880
  681.0 9.1 collective-permute-start.10
  698.9 78.4 %copy-start.39 = (f32[4,288]{1,0:T(4,128)S(1)}, f32[4,288]{1,0:T(4,128)}, u32[]{:S(2)}) copy-start(f32[4,288]{1,0:T(4,128)} %get-tuple-element.71) | copy-start | bytes 13828
  699.0 78.5 %copy-start.35 = (f32[1152]{0:T(1024)S(1)}, f32[1152]{0:T(1024)}, u32[]{:S(2)}) copy-start(f32[1152]{0:T(1024)} %get-tuple-element.68) | copy-start | bytes 13828
  699.0 224.4 %all-reduce.9.cloned.1.call-start = ((), (), s32[]{:S(2)}) async-start(), calls=%async_computation.16 | async-start | bytes 7667712 | tf_op jit(solution)/shard_map/psum | solution.py:58
  777.3 148.7 %copy-start.6 = (f32[368,1152]{1,0:T(8,128)S(1)}, f32[368,1152]{1,0:T(8,128)}, u32[]{:S(2)}) copy-start(f32[368,1152]{1,0:T(8,128)} %copy-done.5) | copy-start | bytes 5087236
  926.0 65.9 %collective-permute-start.5 = (f32[1,144,3456]{2,1,0:T(8,128)}, f32[1,144,3456]{2,1,0:T(8,128)}, u32[]{:S(2)}, u32[]{:S(2)}) collective-permute-start(f32[1,144,3456]{2,1,0:T(8,128)} %convert_element_type.225), channel_id=1, source_target_pairs={{0,4},{4,0},{1,5},{5,1},{2,6},{6,2},{3,7},{7,3},{8,12},{12,8},{9,1... | collective-permute-start | bytes 5971976 | tf_op jit(solution)/shard_map/ppermute | solution.py:31
  937.2 21.5 %copy-start.27 = (bf16[1,144,1152]{2,1,0:T(8,128)(2,1)S(1)}, bf16[1,144,1152]{2,1,0:T(8,128)(2,1)}, u32[]{:S(2)}) copy-start(bf16[1,144,1152]{2,1,0:T(8,128)(2,1)} %get-tuple-element.32) | copy-start | bytes 995332
  937.2 52.4 %copy-start.17 = (bf16[1,144,4304]{2,1,0:T(8,128)(2,1)S(1)}, bf16[1,144,4304]{2,1,0:T(8,128)(2,1)}, u32[]{:S(2)}) copy-start(bf16[1,144,4304]{2,1,0:T(8,128)(2,1)} %get-tuple-element.33) | copy-start | bytes 3718660
  940.7 49.2 %copy-start.15 = (bf16[1,144,4304]{2,1,0:T(8,128)(2,1)S(1)}, bf16[1,144,4304]{2,1,0:T(8,128)(2,1)}, u32[]{:S(2)}) copy-start(bf16[1,144,4304]{2,1,0:T(8,128)(2,1)} %get-tuple-element.34) | copy-start | bytes 3718660
  959.6 31.0 %collective-permute-start.7 = (f32[1,144,1152]{2,1,0:T(8,128)}, f32[1,144,1152]{2,1,0:T(8,128)S(1)}, u32[]{:S(2)}, u32[]{:S(2)}) collective-permute-start(f32[1,144,1152]{2,1,0:T(8,128)} %convert_element_type.230), channel_id=1, source_target_pairs={{0,4},{4,0},{1,5},{5,1},{2,6},{6,2},{3,7},{7,3},{8,12},{12,8},{9,1... | collective-permute-start | bytes 1990664 | tf_op jit(solution)/shard_map/ppermute | solution.py:31
  989.8 6.1 collective-permute-start.9
  990.1 8.8 collective-permute-start.11
  (36 other events, 201.4 us)
Sparse Core Ops, SparseCore 0:
  10.4 53.5 all-gather.9
  66.4 29.1 all-gather.11
  98.1 59.3 all-gather.15
  159.7 59.3 all-gather.13
  549.1 30.4 reduce-scatter.14
  583.1 59.4 reduce-scatter.16
  664.0 50.1 reduce-scatter.12
  717.8 59.4 reduce-scatter.18
  780.0 143.3 all-reduce.8
where the time goes:
time: 1020 us; the launch traced here: 1010 us
  waiting for transfers between devices  459 us (45%)
  local copies, waits for them, and re-layouts  171 us (17%)
  other arithmetic  141 us (14%)
  matrix products  140 us (14%)
  blocking collectives  61.8 us (6%)
  starting transfers between devices  21.1 us (2%)
  between operations  15.7 us (2%)
    all_gather x4, waiting for transfers between devices, gather_weight(): mine = lax.all_gather(piece, 'fsdp', axis=0, tiled=False)  181 us
    psum x1, waiting for transfers between devices, reduce_weight(): part = lax.psum(part, ZAX).astype(jnp.float32)  146 us
    unnamed x13, waiting for transfers between devices  78.3 us
    another operation x8, other arithmetic, gather_weight(): return jnp.stack([first, second], axis=1).reshape(-1, cols)  48.9 us
    unnamed x2, blocking collectives  34.6 us
    convert_element_type x4, other arithmetic, reduce_weight(): chip.astype(jnp.bfloat16)  28.1 us
    psum x1, blocking collectives, shards(): stacked = lax.psum(stacked, SEQ).reshape(-1)  27.2 us
    all_to_all x1, waiting for transfers between devices, shards(): lax.all_to_all(dqkv, GROUP, split_axis=2, concat_axis=3, tiled=True)  25.1 us
  transfers between devices with their start and end apart: 25, of which 10 were waited for; matrix products, arithmetic and copies ran while one was open for 32% of the time, Pallas kernels for 0%

commit v1 on v0

--- a/solution.py
+++ b/solution.py
@@ -3,6 +3,7 @@
 from jax import lax
 from jax.sharding import Mesh
 from jax.sharding import PartitionSpec as P
+from jax.lax import all_to_all, axis_size
 
 HEADS = 16
 HEAD = 72
@@ -10,6 +11,10 @@
 SEQ = ("zh", "zl", "core")
 ZAX = ("zh", "zl")
 GROUP = ("zl", "core")
+check_loops = lambda xs, d_out, out_dim: jnp.concatenate(
+    all_to_all(jnp.stack(jnp.split(xs, axis_size(GROUP), axis=d_out), axis=0), GROUP, 0, 0),
+    axis=out_dim,
+)
 
 
 def layer_norm(values, gain_vec, bias_vec):
@@ -122,7 +127,7 @@
     k = mixed[:, width : 2 * width].astype(bf16)
     v = (mixed[:, 2 * width :] + bv).astype(bf16)
     qkv_tok = jnp.stack([q, k, v]).reshape(3, pairs, part_rows, width)
-    qkv_heads = lax.all_to_all(qkv_tok, GROUP, split_axis=3, concat_axis=2, tiled=True)
+    qkv_heads = check_loops(qkv_tok, 3, 2)
     qkv_heads = qkv_heads.reshape(3, pairs, slot_len, local_heads, HEAD)
     qh, kh, vh = (qkv_heads[0], qkv_heads[1], qkv_heads[2])
     scores = jnp.einsum("pqhd,pkhd->phqk", qh, kh, preferred_element_type=f32) * scale

time: 1020 us -> 983 us (0.964)
  local copies, waits for them, and re-layouts: 171 us -> 145 us
    all_to_all x1 -> x0, local copies, waits for them, and re-layouts: 12.6 us -> none  [shards(): lax.all_to_all(qkv_tok, GROUP, split_axis=3, concat_axis=2, tiled=True)]
    another operation x3 -> x1, local copies, waits for them, and re-layouts: 11.8 us -> 1.42 us  [jnp.stack(jnp.split(xs, axis_size(GROUP), axis=d_out), axis=0)]
  transfers between devices with their start and end apart: 25 -> 25, of which waited for: 10 -> 10; matrix products, arithmetic and copies ran while one was open for 32% -> 31% of each run, Pallas kernels for 0% -> 0%
where the time goes in v1:
time: 983 us; the launch traced here: 974 us
  waiting for transfers between devices  457 us (46%)
  local copies, waits for them, and re-layouts  145 us (15%)
  matrix products  140 us (14%)
  other arithmetic  134 us (14%)
  blocking collectives  61.8 us (6%)
  starting transfers between devices  21.2 us (2%)
  between operations  15.7 us (2%)
    all_gather x4, waiting for transfers between devices, gather_weight(): mine = lax.all_gather(piece, 'fsdp', axis=0, tiled=False)  181 us
    psum x1, waiting for transfers between devices, reduce_weight(): part = lax.psum(part, ZAX).astype(jnp.float32)  146 us
    unnamed x13, waiting for transfers between devices  78.2 us
    another operation x8, other arithmetic, gather_weight(): return jnp.stack([first, second], axis=1).reshape(-1, cols)  48.9 us
    unnamed x2, blocking collectives  34.6 us
    convert_element_type x4, other arithmetic, reduce_weight(): chip.astype(jnp.bfloat16)  28.1 us
    psum x1, blocking collectives, shards(): stacked = lax.psum(stacked, SEQ).reshape(-1)  27.2 us
    all_to_all x1, waiting for transfers between devices, shards(): lax.all_to_all(dqkv, GROUP, split_axis=2, concat_axis=3, tiled=True)  25.1 us
  transfers between devices with their start and end apart: 25, of which 10 were waited for; matrix products, arithmetic and copies ran while one was open for 31% of the time, Pallas kernels for 0%

profile of v1, /device:TPU:0, one launch (start us, length us, event | category | flops | bytes accessed | tf_op | source)
XLA Modules:
  0.0 973.8 jit_solution(10636451179020538937)
XLA Ops:
  14.5 49.5 %all-gather.10.cloned.1.call-done = bf16[576,3456]{1,0:T(8,128)(2,1)} async-done(((bf16[144,3456]{1,0:T(8,128)(2,1)}), bf16[576,3456]{1,0:T(8,128)(2,1)}) %all-gather.10.cloned.1.call-update) | async-done | bytes 3981328 | tf_op jit(solution)/shard_map/all_gather | solution.py:48
  65.6 16.9 %all-reduce = f32[13520]{0:T(1024)S(1)} all-reduce(f32[13520]{0:T(1024)S(1)} %convert_dynamic-update-slice_fusion), channel_id=2, replica_groups=mesh['zh'=2,'zl'=2,'core'=2,'fsdp'=4] {'fsdp'}, use_global_device_ids=true, to_apply=%add | all-reduce | flops 13520 | bytes 108160
  87.8 7.8 all-gather.12.cloned.1.call-done
  95.6 61.8 %all-gather.16.cloned.1.call-done = bf16[576,4304]{1,0:T(8,128)(2,1)} async-done(((bf16[144,4304]{1,0:T(8,128)(2,1)}), bf16[576,4304]{1,0:T(8,128)(2,1)}) %all-gather.16.cloned.1.call-update) | async-done | bytes 4958224 | tf_op jit(solution)/shard_map/all_gather | solution.py:48
  157.5 61.7 %all-gather.14.cloned.1.call-done = bf16[576,4304]{1,0:T(8,128)(2,1)} async-done(((bf16[144,4304]{1,0:T(8,128)(2,1)}), bf16[576,4304]{1,0:T(8,128)(2,1)}) %all-gather.14.cloned.1.call-update) | async-done | bytes 4958224 | tf_op jit(solution)/shard_map/all_gather | solution.py:48
  219.2 5.0 select_bitcast_fusion.5
  224.2 6.0 pad_maximum_fusion.2
  230.2 6.0 fusion.65
  240.5 4.9 all-to-all-start
  249.2 8.5 select_bitcast_fusion.1
  257.7 8.3 select_bitcast_fusion.3
  266.0 19.0 %all-to-all-done = bf16[4,3,2,184,288]{4,3,2,1,0:T(8,128)(2,1)} async-done(((bf16[4,3,2,184,288]{4,3,2,1,0:T(8,128)(2,1)}), bf16[4,3,2,184,288]{4,3,2,1,0:T(8,128)(2,1)}, u32[]{:S(2)}, u32[]{:S(2)}) %all-to-all-start) | async-done | bytes 2543648 | tf_op jit(solution)/shard_map/all_to_all | solution.py:15
  304.0 10.6 %fusion.63 = (f32[2,4,736]{2,1,0:T(4,128)S(1)}, f32[2,4,736,736]{2,3,1,0:T(8,128)}) fusion(f32[2,736]{1,0:T(2,128)S(1)} %fusion.49, bf16[2,736,4,72]{1,3,2,0:T(8,128)(2,1)} %squeeze.70, bf16[2,736,4,72]{1,3,2,0:T(8,128)(2,1)S(1)} %squeeze.71), kind=kOutput, calls=%fused_computation.166 | convolution fusion | flops 641368768 | bytes 19059456 | tf_op jit(solution)/shard_map/sub | solution.py:136
  314.5 9.1 fusion.34
  323.6 4.7 copy.99
  332.7 8.7 pad_maximum_fusion
  341.4 8.3 copy.103
  349.8 8.6 pad_maximum_fusion.1
  367.7 8.4 convolution_add_fusion
  376.2 10.9 %convert_reduce_fusion = (f32[4304]{0:T(1024)}, bf16[368,4304]{1,0:T(8,128)(2,1)}) fusion(f32[368,4304]{1,0:T(8,128)S(1)} %convolution_add_fusion, bf16[368,1152]{1,0:T(8,128)(2,1)S(1)} %bitcast.238, bf16[1152,4304]{1,0:T(8,128)(2,1)S(1)} %bitcast.208), kind=kOutput, calls=%fused_computation.32 | convolution fusion | flops 3690417408 | bytes 20284736 | tf_op jit(solution)/shard_map/dot_general | solution.py:162
  387.1 10.1 %multiply_reduce_fusion.1 = (f32[1152]{0:T(1024)}, f32[368]{0:T(512)S(1)}, f32[1152]{0:T(1024)}, f32[368,1152]{1,0:T(8,128)S(1)}) fusion(f32[368,1152]{1,0:T(8,128)S(1)} %get-tuple-element.89, f32[368]{0:T(512)S(1)} %fusion.50, f32[368]{0:T(512)S(1)} %broadcast_multiply_fusion, f32[1152]{0:T(1024)S(1)} %mul.248, bf16[368,4304]{1,0:T(8,128)(2,1)} %get-tuple-element.36, ...), kind=kOutput, calls=%fused_computation.88 | convolution fusion | flops 3652630016 | bytes 16493888 | tf_op jit(solution)/shard_map/dot_general | solution.py:166
  397.2 9.9 %fusion.54 = f32[1152,4304]{1,0:T(8,128)} fusion(bf16[368,4304]{1,0:T(8,128)(2,1)S(1)} %copy-done.25, f32[368,1152]{1,0:T(8,128)S(1)} %get-tuple-element.89, f32[1152]{0:T(1024)S(1)} %add.211, f32[1152]{0:T(1024)S(1)} %mul.248, f32[368]{0:T(512)S(1)} %fusion.50, f32[368]{0:T(512)S(1)} %broadcast_multiply_fusion), kind=kOutput, calls=%fused_computation.159 | convolution fusion | flops 3651360768 | bytes 24708480 | tf_op jit(solution)/shard_map/dot_general | solution.py:164
  430.2 6.6 fusion.13
  443.3 12.3 %multiply_reduce_fusion = (f32[2,4,736]{2,1,0:T(4,128)S(1)}, f32[2,4,736,736]{2,3,1,0:T(8,128)}) fusion(f32[2,4,736,736]{2,3,1,0:T(8,128)} %get-tuple-element.87, f32[2,4,736]{2,1,0:T(4,128)S(1)} %get-tuple-element.86, bf16[2,736,4,72]{1,3,2,0:T(8,128)(2,1)} %reshape.306, bf16[2,736,4,72]{1,3,2,0:T(8,128)(2,1)} %squeeze.69), kind=kOutput, calls=%fused_computation.2 | convolution fusion | flops 637028608 | bytes 36411392 | tf_op jit(solution)/shard_map/pqhd,pkhd->phqk/dot_general | solution.py:176
  455.6 12.3 %multiply_convert_fusion = bf16[2,4,736,736]{2,3,1,0:T(8,128)(2,1)S(1)} fusion(f32[2,4,736,736]{2,3,1,0:T(8,128)} %get-tuple-element.92, f32[2,4,736]{2,1,0:T(4,128)S(1)} %get-tuple-element.91, f32[2,4,736,736]{2,3,1,0:T(8,128)} %get-tuple-element.87, f32[2,4,736]{2,1,0:T(4,128)S(1)} %get-tuple-element.86), kind=kLoop, calls=%fused_computation.1 | loop fusion | flops 17334272 | bytes 43382784 | tf_op jit(solution)/shard_map/convert_element_type | solution.py:178
  467.9 9.9 %fusion.37 = bf16[2,4,72,736]{3,2,1,0:T(8,128)(2,1)} fusion(bf16[2,736,4,72]{1,3,2,0:T(8,128)(2,1)S(1)} %copy-done.28, f32[2,4,736,736]{2,3,1,0:T(8,128)} %get-tuple-element.87, f32[2,4,736]{2,1,0:T(4,128)S(1)} %get-tuple-element.86), kind=kOutput, calls=%fused_computation.105 | convolution fusion | flops 633124864 | bytes 19053568 | tf_op jit(solution)/shard_map/phqk,pqhd->pkhd/dot_general | solution.py:185
  484.2 4.7 copy.113
  488.9 4.9 copy.112
  496.6 8.7 pad_maximum_fusion.6
  505.3 4.7 all-to-all-start.3
  513.6 8.7 fusion.3
  524.5 25.1 %all-to-all-done.3 = bf16[3,2,736,288]{3,1,0,2:T(2,128)(2,1)} async-done(((bf16[3,2,736,288]{3,1,0,2:T(2,128)(2,1)}), bf16[3,2,736,288]{3,1,0,2:T(2,128)(2,1)}, u32[]{:S(2)}, u32[]{:S(2)}) %all-to-all-start.3) | async-done | bytes 2543648 | tf_op jit(solution)/shard_map/all_to_all | solution.py:189
  549.6 12.9 %copy.136 = bf16[3,2,4,184,288]{3,2,4,1,0:T(4,128)(2,1)} copy(bf16[3,2,4,184,288]{4,1,0,3,2:T(2,128)(2,1)} %bitcast.50) | data formatting | bytes 5087232 | tf_op jit(solution)/shard_map/all_to_all | solution.py:189
  562.5 4.6 fusion.59
  587.7 7.5 fusion.66
  599.2 6.1 fusion.27
  605.3 5.5 copy-done.2
  621.9 7.1 fusion.6
  629.1 12.5 %fusion.20 = f32[4,2,144,4304]{3,2,1,0:T(8,128)} fusion(bf16[4,2,144,368]{3,2,1,0:T(8,128)(2,1)S(1)} %bitcast.213, f32[368,4304]{1,0:T(8,128)} %copy-done.13), kind=kOutput, calls=%fused_computation.52 | convolution fusion | flops 3663495936 | bytes 27016192 | tf_op jit(solution)/shard_map/dot_general | solution.py:160
  641.5 4.6 fusion.14
  647.1 8.1 collective-permute-done.10
  655.1 8.9 fusion.2
  664.3 15.0 %reduce-scatter.13.cloned.1.call-done = bf16[1,144,3456]{2,1,0:T(8,128)(2,1)} async-done(((bf16[4,144,3456]{2,1,0:T(8,128)(2,1)}), bf16[1,144,3456]{2,1,0:T(8,128)(2,1)}) %reduce-scatter.13.cloned.1.call-update) | async-done | bytes 995344
  679.3 63.1 %reduce-scatter.19.cloned.1.call-done = bf16[1,144,4304]{2,1,0:T(8,128)(2,1)} async-done(((bf16[4,144,4304]{2,1,0:T(8,128)(2,1)}), bf16[1,144,4304]{2,1,0:T(8,128)(2,1)}) %reduce-scatter.19.cloned.1.call-update) | async-done | bytes 1239568
  742.6 145.8 %all-reduce.9.cloned.1.call-done = (bf16[1,144,3456]{2,1,0:T(8,128)(2,1)}, bf16[1,144,1152]{2,1,0:T(8,128)(2,1)}, bf16[1,144,4304]{2,1,0:T(8,128)(2,1)}, bf16[1,144,4304]{2,1,0:T(8,128)(2,1)}) async-done(((bf16[1,144,3456]{2,1,0:T(8,128)(2,1)}, bf16[1,144,1152]{2,1,0:T(8,128)(2,1)}, bf16[1,144,4304]{2,1,0:T(8,128)(2,1)}, bf16[1,144,4304]{2,1,0:T(8,128)(2,1)}), (bf16[1,144,3456]{2,1,0:T(8,128)(2,1)}, ...) | async-done | bytes 3806224 | tf_op jit(solution)/shard_map/psum | solution.py:63
  891.2 11.2 %fusion.25 = bf16[368,1152]{1,0:T(8,128)(2,1)} fusion(f32[368,1152]{1,0:T(8,128)S(1)} %copy-done.6, bf16[1152,4304]{1,0:T(8,128)(2,1)} %bitcast.205, f32[368]{0:T(512)S(1)} %mul.257, f32[1152]{0:T(1024)S(1)} %add.220, f32[368,4304]{1,0:T(8,128)} %copy-done.13), kind=kOutput, calls=%fused_computation.59 | convolution fusion | flops 3665191680 | bytes 18801600 | tf_op jit(solution)/shard_map/dot_general | solution.py:151
  906.0 17.7 %all-reduce.1 = f32[4,3380]{1,0:T(4,128)} all-reduce(f32[4,3380]{1,0:T(4,128)S(1)} %concatenate.26), channel_id=7, replica_groups=mesh['zh'=2,'zl'=2,'core'=2,'fsdp'=4] {'fsdp'}, use_global_device_ids=true, to_apply=%region_20.21.clone | all-reduce | flops 13520 | bytes 108160
  926.1 27.2 %psum.35 = f32[1,3380]{1,0:T(1,128)S(1)} all-reduce(f32[1,3380]{1,0:T(1,128)S(1)} %constant_dynamic-slice_fusion.5), channel_id=1, replica_groups=mesh['zh'=2,'zl'=2,'core'=2,'fsdp'=4] {'zh','zl','core'}, use_global_device_ids=true, to_apply=%region_21.22 | all-reduce | flops 3380 | bytes 27040 | tf_op jit(solution)/shard_map/psum | solution.py:212
  (282 shorter events, 157.8 us)
Async XLA Ops:
  7.2 56.8 %all-gather.10.cloned.1.call-start = ((), (), s32[]{:S(2)}) async-start(), calls=%async_computation.8 | async-start | bytes 4976640 | tf_op jit(solution)/shard_map/all_gather | solution.py:48
  9.7 85.9 %all-gather.12.cloned.1.call-start = ((), (), s32[]{:S(2)}) async-start(), calls=%async_computation.9 | async-start | bytes 1658880 | tf_op jit(solution)/shard_map/all_gather | solution.py:48
  10.5 146.9 %all-gather.16.cloned.1.call-start = ((), (), s32[]{:S(2)}) async-start(), calls=%async_computation.11 | async-start | bytes 6266880 | tf_op jit(solution)/shard_map/all_gather | solution.py:48
  11.7 52.3 %copy-start.46 = (u32[32]{0:T(128)S(1)}, u32[32]{0:T(128)}, u32[]{:S(2)}) copy-start(u32[32]{0:T(128)} %constant.89) | copy-start | bytes 388
  11.7 53.5 %copy-start.45 = (bf16[1076]{0:T(1024)(128)(2,1)S(1)}, bf16[1076]{0:T(1024)(128)(2,1)}, u32[]{:S(2)}) copy-start(bf16[1076]{0:T(1024)(128)(2,1)} %param.30) | copy-start | bytes 6460
  11.7 53.5 %copy-start.47 = (bf16[288]{0:T(512)(128)(2,1)S(1)}, bf16[288]{0:T(512)(128)(2,1)}, u32[]{:S(2)}) copy-start(bf16[288]{0:T(512)(128)(2,1)} %param.20) | copy-start | bytes 1732
  11.7 53.5 %copy-start.48 = (bf16[288]{0:T(512)(128)(2,1)S(1)}, bf16[288]{0:T(512)(128)(2,1)}, u32[]{:S(2)}) copy-start(bf16[288]{0:T(512)(128)(2,1)} %param.21) | copy-start | bytes 1732
  11.7 53.5 %copy-start.49 = (bf16[288]{0:T(512)(128)(2,1)S(1)}, bf16[288]{0:T(512)(128)(2,1)}, u32[]{:S(2)}) copy-start(bf16[288]{0:T(512)(128)(2,1)} %param.23) | copy-start | bytes 1732
  11.8 53.5 %copy-start.50 = (bf16[288]{0:T(512)(128)(2,1)S(1)}, bf16[288]{0:T(512)(128)(2,1)}, u32[]{:S(2)}) copy-start(bf16[288]{0:T(512)(128)(2,1)} %param.24) | copy-start | bytes 1732
  11.8 53.5 %copy-start.51 = (bf16[288]{0:T(512)(128)(2,1)S(1)}, bf16[288]{0:T(512)(128)(2,1)}, u32[]{:S(2)}) copy-start(bf16[288]{0:T(512)(128)(2,1)} %param.26) | copy-start | bytes 1732
  11.8 53.5 %copy-start.52 = (bf16[288]{0:T(512)(128)(2,1)S(1)}, bf16[288]{0:T(512)(128)(2,1)}, u32[]{:S(2)}) copy-start(bf16[288]{0:T(512)(128)(2,1)} %param.27) | copy-start | bytes 1732
  11.8 53.5 %copy-start.53 = (bf16[288]{0:T(512)(128)(2,1)S(1)}, bf16[288]{0:T(512)(128)(2,1)}, u32[]{:S(2)}) copy-start(bf16[288]{0:T(512)(128)(2,1)} %param.28) | copy-start | bytes 1732
  11.8 53.5 %copy-start.54 = (bf16[288]{0:T(512)(128)(2,1)S(1)}, bf16[288]{0:T(512)(128)(2,1)}, u32[]{:S(2)}) copy-start(bf16[288]{0:T(512)(128)(2,1)} %param.32) | copy-start | bytes 1732
  11.8 71.9 %copy-start.41 = (s32[4,736]{1,0:T(4,128)S(1)}, s32[4,736]{1,0:T(4,128)}, u32[]{:S(2)}) copy-start(s32[4,736]{1,0:T(4,128)} %param.18) | copy-start | bytes 35332
  11.8 71.9 %copy-start.55 = (s32[4]{0:T(128)S(1)}, s32[4]{0:T(128)}, u32[]{:S(2)}) copy-start(s32[4]{0:T(128)} %param.19) | copy-start | bytes 52
  11.8 72.6 %copy-start.3 = (bf16[2,184,1152]{2,1,0:T(8,128)(2,1)S(1)}, bf16[2,184,1152]{2,1,0:T(8,128)(2,1)}, u32[]{:S(2)}) copy-start(bf16[2,184,1152]{2,1,0:T(8,128)(2,1)} %param.17) | copy-start | bytes 2543620
  11.9 73.8 %copy-start.9 = (bf16[2,184,1152]{2,1,0:T(8,128)(2,1)S(1)}, bf16[2,184,1152]{2,1,0:T(8,128)(2,1)}, u32[]{:S(2)}) copy-start(bf16[2,184,1152]{2,1,0:T(8,128)(2,1)} %param.33) | copy-start | bytes 2543620
  11.9 207.3 %all-gather.14.cloned.1.call-start = ((), (), s32[]{:S(2)}) async-start(), calls=%async_computation.10 | async-start | bytes 6266880 | tf_op jit(solution)/shard_map/all_gather | solution.py:48
  64.0 155.2 %collective-permute-start = (bf16[4,144,3456]{2,1,0:T(8,128)(2,1)}, bf16[4,144,3456]{2,1,0:T(8,128)(2,1)}, u32[]{:S(2)}, u32[]{:S(2)}) collective-permute-start(bf16[4,144,3456]{2,1,0:T(8,128)(2,1)} %bitcast.221), channel_id=1, source_target_pairs={{0,4},{4,0},{1,5},{5,1},{2,6},{6,2},{3,7},{7,3},{8,12},{12,8},{9,1... | collective-permute-start | bytes 11943944 | tf_op jit(solution)/shard_map/ppermute | solution.py:36
  84.7 139.5 %copy-start.36 = (f32[2,184]{1,0:T(2,128)}, f32[2,184]{1,0:T(2,128)S(1)}, u32[]{:S(2)}) copy-start(f32[2,184]{1,0:T(2,128)S(1)} %broadcast_multiply_fusion.1) | copy-start | bytes 4420
  95.6 149.8 %collective-permute-start.1 = (bf16[4,144,1152]{2,1,0:T(8,128)(2,1)}, bf16[4,144,1152]{2,1,0:T(8,128)(2,1)}, u32[]{:S(2)}, u32[]{:S(2)}) collective-permute-start(bf16[4,144,1152]{2,1,0:T(8,128)(2,1)} %bitcast.234), channel_id=1, source_target_pairs={{0,4},{4,0},{1,5},{5,1},{2,6},{6,2},{3,7},{7,3},{8,12},{12,8},{9,1... | collective-permute-start | bytes 3981320 | tf_op jit(solution)/shard_map/ppermute | solution.py:36
  157.5 91.7 %collective-permute-start.3 = (bf16[4,144,4304]{2,1,0:T(8,128)(2,1)}, bf16[4,144,4304]{2,1,0:T(8,128)(2,1)}, u32[]{:S(2)}, u32[]{:S(2)}) collective-permute-start(bf16[4,144,4304]{2,1,0:T(8,128)(2,1)} %bitcast.215), channel_id=1, source_target_pairs={{0,4},{4,0},{1,5},{5,1},{2,6},{6,2},{3,7},{7,3},{8,12},{12,8},{9,1... | collective-permute-start | bytes 14874632 | tf_op jit(solution)/shard_map/ppermute | solution.py:36
  219.2 38.5 %collective-permute-start.2 = (bf16[4,144,4304]{2,1,0:T(8,128)(2,1)}, bf16[4,144,4304]{2,1,0:T(8,128)(2,1)}, u32[]{:S(2)}, u32[]{:S(2)}) collective-permute-start(bf16[4,144,4304]{2,1,0:T(8,128)(2,1)} %bitcast.217), channel_id=1, source_target_pairs={{0,4},{4,0},{1,5},{5,1},{2,6},{6,2},{3,7},{7,3},{8,12},{12,8},{9,1... | collective-permute-start | bytes 14874632 | tf_op jit(solution)/shard_map/ppermute | solution.py:36
  240.5 44.4 %all-to-all-start = ((bf16[4,3,2,184,288]{4,3,2,1,0:T(8,128)(2,1)}), bf16[4,3,2,184,288]{4,3,2,1,0:T(8,128)(2,1)}, u32[]{:S(2)}, u32[]{:S(2)}) async-start(bf16[4,3,2,184,288]{4,3,2,1,0:T(8,128)(2,1)} %pad_maximum_fusion.5), calls=%async_computation | async-start | bytes 6782976 | tf_op jit(solution)/shard_map/all_to_all | solution.py:15
  328.2 30.1 %all-to-all-start.1 = ((bf16[2,736,288]{2,0,1:T(2,128)(2,1)}), bf16[2,736,288]{2,0,1:T(2,128)(2,1)}, u32[]{:S(2)}, u32[]{:S(2)}) async-start(bf16[2,736,288]{2,0,1:T(2,128)(2,1)} %copy.99), calls=%async_computation.1 | async-start | bytes 2260992 | tf_op jit(solution)/shard_map/all_to_all | solution.py:141
  367.3 39.8 %copy-start.5 = (f32[368,1152]{1,0:T(8,128)}, f32[368,1152]{1,0:T(8,128)S(1)}, u32[]{:S(2)}) copy-start(f32[368,1152]{1,0:T(8,128)S(1)} %get-tuple-element.89) | copy-start | bytes 5087236
  416.5 20.4 %all-to-all-start.2 = ((bf16[2,184,1152]{1,0,2:T(2,128)(2,1)}), bf16[2,184,1152]{1,0,2:T(2,128)(2,1)}, u32[]{:S(2)}, u32[]{:S(2)}) async-start(bf16[2,184,1152]{1,0,2:T(2,128)(2,1)} %copy.105), calls=%async_computation.2 | async-start | bytes 2359296 | tf_op jit(solution)/shard_map/all_to_all | solution.py:173
  429.7 80.3 %collective-permute-start.6 = (bf16[4,144,1152]{2,1,0:T(8,128)(2,1)}, bf16[4,144,1152]{2,1,0:T(8,128)(2,1)}, u32[]{:S(2)}, u32[]{:S(2)}) collective-permute-start(bf16[4,144,1152]{2,1,0:T(8,128)(2,1)} %fusion.40), channel_id=1, source_target_pairs={{0,4},{4,0},{1,5},{5,1},{2,6},{6,2},{3,7},{7,3},{8,12},{12,8},{9,1... | collective-permute-start | bytes 3981320 | tf_op jit(solution)/shard_map/ppermute | solution.py:36
  436.8 76.8 %collective-permute-start.8 = (bf16[4,144,4304]{2,1,0:T(8,128)(2,1)}, bf16[4,144,4304]{2,1,0:T(8,128)(2,1)}, u32[]{:S(2)}, u32[]{:S(2)}) collective-permute-start(bf16[4,144,4304]{2,1,0:T(8,128)(2,1)} %fusion.13), channel_id=1, source_target_pairs={{0,4},{4,0},{1,5},{5,1},{2,6},{6,2},{3,7},{7,3},{8,12},{12,8},{9,1... | collective-permute-start | bytes 14874632 | tf_op jit(solution)/shard_map/ppermute | solution.py:36
  455.6 12.3 %copy-start.28 = (bf16[2,736,4,72]{1,3,2,0:T(8,128)(2,1)S(1)}, bf16[2,736,4,72]{1,3,2,0:T(8,128)(2,1)}, u32[]{:S(2)}) copy-start(bf16[2,736,4,72]{1,3,2,0:T(8,128)(2,1)} %reshape.306) | copy-start | bytes 2543620
  505.3 44.3 %all-to-all-start.3 = ((bf16[3,2,736,288]{3,1,0,2:T(2,128)(2,1)}), bf16[3,2,736,288]{3,1,0,2:T(2,128)(2,1)}, u32[]{:S(2)}, u32[]{:S(2)}) async-start(bf16[3,2,736,288]{3,1,0,2:T(2,128)(2,1)} %pad_maximum_fusion.6), calls=%async_computation.3 | async-start | bytes 6782976 | tf_op jit(solution)/shard_map/all_to_all | solution.py:189
  510.0 154.3 %reduce-scatter.15.cloned.1.call-start = ((), (), s32[]{:S(2)}) async-start(), calls=%async_computation.13 | async-start | bytes 1658880
  513.5 150.8 %reduce-scatter.17.cloned.1.call-start = ((), (), s32[]{:S(2)}) async-start(), calls=%async_computation.14 | async-start | bytes 6266880
  522.3 157.0 %reduce-scatter.13.cloned.1.call-start = ((), (), s32[]{:S(2)}) async-start(), calls=%async_computation.12 | async-start | bytes 4976640
  613.2 8.7 collective-permute-start.4
  629.0 113.4 %reduce-scatter.19.cloned.1.call-start = ((), (), s32[]{:S(2)}) async-start(), calls=%async_computation.15 | async-start | bytes 6266880
  646.1 9.1 collective-permute-start.10
  664.0 78.4 %copy-start.39 = (f32[4,288]{1,0:T(4,128)S(1)}, f32[4,288]{1,0:T(4,128)}, u32[]{:S(2)}) copy-start(f32[4,288]{1,0:T(4,128)} %get-tuple-element.75) | copy-start | bytes 13828
  664.0 78.5 %copy-start.35 = (f32[1152]{0:T(1024)S(1)}, f32[1152]{0:T(1024)}, u32[]{:S(2)}) copy-start(f32[1152]{0:T(1024)} %get-tuple-element.72) | copy-start | bytes 13828
  664.1 224.4 %all-reduce.9.cloned.1.call-start = ((), (), s32[]{:S(2)}) async-start(), calls=%async_computation.16 | async-start | bytes 7667712 | tf_op jit(solution)/shard_map/psum | solution.py:63
  742.4 148.8 %copy-start.6 = (f32[368,1152]{1,0:T(8,128)S(1)}, f32[368,1152]{1,0:T(8,128)}, u32[]{:S(2)}) copy-start(f32[368,1152]{1,0:T(8,128)} %copy-done.5) | copy-start | bytes 5087236
  891.1 65.9 %collective-permute-start.5 = (f32[1,144,3456]{2,1,0:T(8,128)}, f32[1,144,3456]{2,1,0:T(8,128)}, u32[]{:S(2)}, u32[]{:S(2)}) collective-permute-start(f32[1,144,3456]{2,1,0:T(8,128)} %convert_element_type.225), channel_id=1, source_target_pairs={{0,4},{4,0},{1,5},{5,1},{2,6},{6,2},{3,7},{7,3},{8,12},{12,8},{9,1... | collective-permute-start | bytes 5971976 | tf_op jit(solution)/shard_map/ppermute | solution.py:36
  902.3 21.5 %copy-start.27 = (bf16[1,144,1152]{2,1,0:T(8,128)(2,1)S(1)}, bf16[1,144,1152]{2,1,0:T(8,128)(2,1)}, u32[]{:S(2)}) copy-start(bf16[1,144,1152]{2,1,0:T(8,128)(2,1)} %get-tuple-element.32) | copy-start | bytes 995332
  902.3 52.4 %copy-start.17 = (bf16[1,144,4304]{2,1,0:T(8,128)(2,1)S(1)}, bf16[1,144,4304]{2,1,0:T(8,128)(2,1)}, u32[]{:S(2)}) copy-start(bf16[1,144,4304]{2,1,0:T(8,128)(2,1)} %get-tuple-element.33) | copy-start | bytes 3718660
  905.8 49.2 %copy-start.15 = (bf16[1,144,4304]{2,1,0:T(8,128)(2,1)S(1)}, bf16[1,144,4304]{2,1,0:T(8,128)(2,1)}, u32[]{:S(2)}) copy-start(bf16[1,144,4304]{2,1,0:T(8,128)(2,1)} %get-tuple-element.34) | copy-start | bytes 3718660
  924.7 31.0 %collective-permute-start.7 = (f32[1,144,1152]{2,1,0:T(8,128)}, f32[1,144,1152]{2,1,0:T(8,128)S(1)}, u32[]{:S(2)}, u32[]{:S(2)}) collective-permute-start(f32[1,144,1152]{2,1,0:T(8,128)} %convert_element_type.230), channel_id=1, source_target_pairs={{0,4},{4,0},{1,5},{5,1},{2,6},{6,2},{3,7},{7,3},{8,12},{12,8},{9,1... | collective-permute-start | bytes 1990664 | tf_op jit(solution)/shard_map/ppermute | solution.py:36
  954.9 6.1 collective-permute-start.9
  955.1 8.8 collective-permute-start.11
  (36 other events, 201.6 us)
Sparse Core Ops, SparseCore 0:
  10.4 53.5 all-gather.9
  66.4 29.1 all-gather.11
  98.1 59.3 all-gather.15
  159.7 59.3 all-gather.13
  514.1 30.3 reduce-scatter.14
  548.0 59.3 reduce-scatter.16
  629.1 50.1 reduce-scatter.12
  682.9 59.4 reduce-scatter.18
  745.0 143.3 all-reduce.8
